TPU v7x, 32 devices: a whole 2x2x4 slice. The times are simulated.
32 devices in a mesh: virt: 8 (over z, x), aux: 4 (over y, core).
Axes of the slice: x: 2, y: 2, z: 4, core: 2. Of those that a mesh axis runs over, the one named last changes fastest.
Arguments:
- three_index: bfloat16 [600, 5120], P('aux', 'virt'), may hold values from -0.0625 to 0.0625
- eps_occ: float32 [20], replicated, may hold values from -1.5 to -0.5
- eps_virt: float32 [256], replicated, may hold values from 0.3 to 3
Outputs:
- virt_energy: float32 [256], P('virt')
- pair_energy: float32 [20, 20], replicated
All inputs are finite; a program needn't handle non-finite values.
Results may differ from a plain program's by a relative error of at most 0.0003.
Values may be sent and summed in bfloat16 or wider, within the bound.
A program may use at most 128 MiB of HBM per device.

v0:
```python
import jax
import jax.numpy as jnp
from jax import lax
from jax.sharding import PartitionSpec as P


def on_device(three_index, eps_occ, eps_virt):
    occupied = eps_occ.shape[0]
    own_width = three_index.shape[1] // occupied
    virt_count = lax.axis_size("virt")
    aux_place = lax.axis_index("aux")
    virt_place = lax.axis_index("virt")
    narrow = lax.all_to_all(three_index, "aux", split_axis=1, concat_axis=0, tiled=True)
    partner = lax.all_gather(narrow, "virt", axis=1, tiled=True)
    stride = narrow.shape[1] // occupied
    table = eps_virt.reshape(virt_count, own_width)
    eps_other = lax.dynamic_slice_in_dim(table, aux_place * stride, stride, 1).reshape(-1)
    other_width = partner.shape[1] // occupied
    partner_cube = partner.reshape(partner.shape[0], other_width, occupied)
    eps_own = lax.dynamic_slice_in_dim(eps_virt, virt_place * own_width, own_width)
    incoming = lax.all_gather(three_index, "aux", axis=0, tiled=True)
    rows = incoming.shape[0]
    left_cube = incoming.reshape(rows, own_width, occupied)
    integrals = jnp.einsum(
        "pai,pbj->iajb", left_cube, partner_cube, preferred_element_type=jnp.float32
    )
    denominator = (
        eps_occ[:, None, None, None]
        + eps_occ[None, None, :, None]
        - eps_own[None, :, None, None]
        - eps_other[None, None, None, :]
    )
    swapped = jnp.transpose(integrals, (2, 1, 0, 3))
    energy_terms = integrals * (2.0 * integrals - swapped) / denominator
    virt_local = jnp.sum(energy_terms, axis=(0, 2, 3))
    pair_local = jnp.sum(energy_terms, axis=(1, 3))
    virt_energy, pair_column = lax.psum((virt_local, pair_local), "aux")
    pair_energy = lax.psum(pair_column, "virt")
    return (virt_energy, pair_energy)


def solution(mesh):
    in_specs = (P("aux", "virt"), P(), P())
    out_specs = (P("virt"), P())
    return jax.shard_map(
        on_device, mesh=mesh, in_specs=in_specs, out_specs=out_specs, check_vma=False
    )
```

profile of v0, /device:TPU:0, one launch (start us, length us, event | category | flops | bytes accessed | tf_op | source)
XLA Modules:
  0.0 129.4 jit_solution(3256470533484505875)
XLA Ops:
  7.2 0.0 copy-start
  7.2 0.0 all-gather.3.cloned.1.call-start
  7.2 1.2 all_to_all.14
  8.4 10.6 %all_to_all.19 = bf16[150,4,160]{2,0,1:T(8,128)(2,1)S(1)} all-to-all(bf16[150,4,160]{2,0,1:T(8,128)(2,1)S(1)} %copy.16), channel_id=1, replica_groups=mesh['virt'=8,'aux'=4] {'aux'}, dimensions={1} | all-to-all | bytes 384000 | tf_op jit(solution)/shard_map/all_to_all | solution.py:13
  19.0 0.1 reshape.63
  19.1 0.8 copy.23
  20.0 0.0 all-gather.3.cloned.1.call-update
  20.0 0.8 reshape.57
  20.8 0.8 dynamic_slice.6
  21.5 0.1 constant_dynamic-slice_fusion
  21.6 0.1 sub.41
  21.7 8.4 %all-gather = bf16[4,150,640]{2,1,0:T(8,128)(2,1)S(1)} all-gather(bf16[1,150,640]{2,1,0:T(8,128)(2,1)} %bitcast.31), channel_id=1, replica_groups=mesh['virt'=8,'aux'=4] {'aux'}, dimensions={0}, use_global_device_ids=true | all-gather | bytes 960000 | tf_op jit(solution)/shard_map/all_gather | solution.py:21
  30.0 1.2 copy.18
  31.3 1.1 reshape.56
  32.4 0.0 copy-done
  32.4 0.1 broadcast_add_fusion
  32.5 0.1 broadcast_subtract_fusion
  32.6 32.6 %all-gather.3.cloned.1.call-done = bf16[600,1280]{0,1:T(8,128)(2,1)} async-done(((bf16[600,160]{0,1:T(8,128)(2,1)}), bf16[600,1280]{0,1:T(8,128)(2,1)}) %all-gather.3.cloned.1.call-update) | async-done | bytes 1536016 | tf_op jit(solution)/shard_map/all_gather | solution.py:14
  65.3 2.7 %reshape.55 = bf16[600,64,20]{0,2,1:T(8,128)(2,1)S(1)} reshape(bf16[600,1280]{0,1:T(8,128)(2,1)} %all-gather.3.cloned.1.call-done) | data formatting | bytes 3072000 | tf_op jit(solution)/shard_map/reshape | solution.py:19
  67.9 2.7 %fusion.2 = f32[64,20,32,20]{0,2,3,1:T(8,128)S(1)} fusion(bf16[600,64,20,1]{0,2,1,3:T(8,128)(2,1)S(1)} %bitcast.29, bf16[600,32,20]{0,2,1:T(8,128)(2,1)S(1)} %reshape.56), kind=kOutput, calls=%fused_computation.4 | convolution fusion | flops 983040000 | bytes 5580800 | tf_op jit(solution)/shard_map/pai,pbj->iajb/dot_general | solution.py:24
  70.7 6.5 %fusion.6 = (f32[20,20]{1,0:T(8,128)S(1)}, f32[32]{0:T(128)S(1)}) fusion(f32[64]{0:T(128)S(1)} %sub.41, f32[20,32,20]{1,2,0:T(8,128)S(1)} %broadcast_subtract_fusion, f32[64,20,32,20]{0,2,3,1:T(8,128)S(1)} %fusion.2), kind=kLoop, calls=%fused_computation.8 | loop fusion | flops 5733968 | bytes 3329984 | tf_op jit(solution)/shard_map/reduce_sum | solution.py:36
  77.2 10.6 %all-reduce = (f32[32]{0:T(128)}, f32[20,20]{1,0:T(8,128)S(1)}) all-reduce(f32[32]{0:T(128)S(1)} %get-tuple-element.3, f32[20,20]{1,0:T(8,128)S(1)} %get-tuple-element.2), channel_id=1, replica_groups=mesh['virt'=8,'aux'=4] {'aux'}, use_global_device_ids=true, to_apply=%region_1.0 | all-reduce | flops 432 | bytes 3456 | tf_op jit(solution)/shard_map/psum | solution.py:37
  87.8 34.8 %psum.23 = f32[20,20]{1,0:T(8,128)} all-reduce(f32[20,20]{1,0:T(8,128)S(1)} %get-tuple-element.5), channel_id=1, replica_groups=mesh['virt'=8,'aux'=4] {'virt'}, use_global_device_ids=true, to_apply=%region_4.0 | all-reduce | flops 400 | bytes 3200 | tf_op jit(solution)/shard_map/psum | solution.py:38
  (1 shorter events, 0.0 us)
Async XLA Ops:
  7.2 25.2 %copy-start = (f32[20]{0:T(128)S(1)}, f32[20]{0:T(128)}, u32[]{:S(2)}) copy-start(f32[20]{0:T(128)} %param.4) | copy-start | bytes 244
  7.2 58.1 %all-gather.3.cloned.1.call-start = ((), (), s32[]{:S(2)}) async-start(), calls=%async_computation.1 | async-start | bytes 1843200 | tf_op jit(solution)/shard_map/all_gather | solution.py:14
Sparse Core Ops, SparseCore 0:
  20.1 45.0 all-gather.2
where the time goes:
time: 130 us; the launch traced here: 129 us
  blocking collectives  64.4 us (50%)
  waiting for transfers between devices  32.7 us (25%)
  between operations  14.1 us (11%)
  local copies, waits for them, and re-layouts  8.83 us (7%)
  other arithmetic  6.69 us (5%)
  matrix products  2.73 us (2%)
    psum x1, blocking collectives, on_device(): pair_energy = lax.psum(pair_column, 'virt')  34.8 us
    all_gather x1, waiting for transfers between devices, on_device(): partner = lax.all_gather(narrow, 'virt', axis=1, tiled=True)  32.6 us
    psum x1, blocking collectives, on_device(): virt_energy, pair_column = lax.psum((virt_local, pair_local), 'aux')  10.6 us
    all_to_all x1, blocking collectives, on_device(): lax.all_to_all(three_index, 'aux', split_axis=1, concat_axis=0, tiled=True)  10.6 us
    all_gather x1, blocking collectives, on_device(): incoming = lax.all_gather(three_index, 'aux', axis=0, tiled=True)  8.36 us
    reduce_sum x1, other arithmetic, on_device(): pair_local = jnp.sum(energy_terms, axis=(1, 3))  6.49 us
    dot_general x1, matrix products, on_device(): jnp.einsum('pai,pbj->iajb', left_cube, partner_cube, preferred_element_ty...  2.73 us
    reshape x1, local copies, waits for them, and re-layouts, on_device(): partner_cube = partner.reshape(partner.shape[0], other_width, occupied)  2.67 us
  transfers between devices with their start and end apart: 1, of which 1 were waited for; matrix products, arithmetic and copies ran while one was open for 3% of the time, Pallas kernels for 0%

commit v1 on v0

v1 whole, which is shorter than its diff:
```python
import functools

import jax
import jax.numpy as jnp
from jax import lax
from jax.experimental import pallas as pl
from jax.experimental.pallas import tpu as pltpu
from jax.sharding import PartitionSpec as P

MESH = pl.DeviceIdType.MESH
F32 = jnp.float32
BF16 = jnp.bfloat16
EXACT = lax.Precision.HIGHEST
LANES = 128
NT = (((1,), (1,)), ((), ()))
NN = (((1,), (0,)), ((), ()))


def distances(n_aux):
    return list(range(1, n_aux + 1, 2)) + list(range(2, n_aux + 1, 2))


def pick(table, at):
    got = jnp.int32(table[0])
    for k in range(1, len(table)):
        got = jnp.where(at == k, jnp.int32(table[k]), got)
    return got


def label_of(virt, n_virt):
    return lax.rem(virt, 2) * (n_virt // 2) + virt // 2


def virt_of(label, n_virt):
    half = n_virt // 2
    return lax.rem(label, half) * 2 + label // half


def kernel(
    n_virt, n_aux, occ,
    x_ref, occ_ref, virt_ref,
    share_ref, pair_ref,
    held, lhs, rhs, order, ints, sums, parts, message, slots,
    own_sem, send_sem, recv_sem, msg_send, msg_recv,
):
    rows, cols = x_ref.shape
    width = cols // occ
    groups = LANES // width
    supers = occ // groups
    n = n_virt * n_aux
    v = lax.axis_index("virt")
    p = lax.axis_index("aux")
    me = v * n_aux + p
    table = distances(n_aux)
    label = label_of(v, n_virt)
    other = virt_of(lax.rem(label + pick(table, p), n_virt), n_virt)
    diag = jnp.logical_and(p == n_aux - 1, label >= n_virt // 2)

    barrier = pltpu.get_barrier_semaphore()

    def greet(k, c):
        t = lax.rem(me + k, n)
        pl.semaphore_signal(
            barrier, inc=1,
            device_id={"virt": t // n_aux, "aux": lax.rem(t, n_aux)},
            device_id_type=MESH,
        )
        return c

    lax.fori_loop(1, n, greet, 0)
    own = pltpu.make_async_copy(x_ref, held.at[0, p], own_sem)
    own.start()
    pl.semaphore_wait(barrier, n - 1)

    copies = []
    for k in range(n_aux):
        q = lax.rem(p + k, n_aux)
        target = virt_of(lax.rem(label + n_virt - pick(table, q), n_virt), n_virt)
        copies.append(pltpu.make_async_remote_copy(
            src_ref=x_ref, dst_ref=held.at[1, p],
            send_sem=send_sem.at[1, k], recv_sem=recv_sem.at[1, p],
            device_id={"virt": target, "aux": q}, device_id_type=MESH,
        ))
    for k in range(1, n_aux):
        q = lax.rem(p + k, n_aux)
        copies.append(pltpu.make_async_remote_copy(
            src_ref=x_ref, dst_ref=held.at[0, p],
            send_sem=send_sem.at[0, k], recv_sem=recv_sem.at[0, p],
            device_id={"virt": v, "aux": q}, device_id_type=MESH,
        ))
    for copy in copies:
        copy.start()

    def arrived(side, q):
        pltpu.make_async_copy(
            held.at[side, q], held.at[side, q], recv_sem.at[side, q]
        ).wait()

    row = lax.broadcasted_iota(jnp.int32, (cols, cols), 0)
    col = lax.broadcasted_iota(jnp.int32, (cols, cols), 1)
    hit = col == lax.rem(row, width) * occ + row // width
    order[...] = jnp.where(hit, 1.0, 0.0).astype(BF16)
    lhs[...] = jnp.zeros_like(lhs)
    rhs[...] = jnp.zeros_like(rhs)

    def turn(side, q):
        lhs[q, :, 0:rows] = lax.dot_general(
            order[...], held[side, q], NT, preferred_element_type=F32
        ).astype(BF16)

    own.wait()
    turn(0, p)

    def take(k, c):
        q = lax.rem(p + k, n_aux)
        arrived(0, q)
        turn(0, q)
        return c

    lax.fori_loop(1, n_aux, take, 0)

    lane = lax.broadcasted_iota(jnp.int32, (1, LANES), 1)
    part = lane // width
    down = lax.broadcasted_iota(jnp.int32, (width, 1), 0)
    lane_in = lax.rem(lane, width)

    def eps_down(which):
        got = jnp.zeros((width, 1), F32)
        for k in range(width):
            got = jnp.where(down == k, virt_ref[which * width + k], got)
        return got

    def eps_across(which):
        got = jnp.zeros((1, LANES), F32)
        for k in range(width):
            got = jnp.where(lane_in == k, virt_ref[which * width + k], got)
        return got

    occ_lane = []
    for cj in range(supers):
        got = jnp.zeros((1, LANES), F32)
        for t in range(groups):
            got = jnp.where(part == t, occ_ref[cj * groups + t], got)
        occ_lane.append(got)

    tall = -(-occ // 8)
    sums[...] = jnp.zeros_like(sums)
    n_tiles = jnp.where(diag, 2, 1)
    r8 = lax.broadcasted_iota(jnp.int32, (8, LANES), 0)
    l8 = lax.broadcasted_iota(jnp.int32, (8, LANES), 1)
    free = tall * width

    def tile(t, c):
        last = t == n_tiles - 1
        source = jnp.where(diag, t, 1)

        def step(k, c2):
            q = lax.rem(p + k, n_aux)

            @pl.when(last)
            def _():
                arrived(1, q)

            @pl.when(t == 1)
            def _():
                turn(1, q)

            rhs[0:rows, :] = lax.dot_general(
                held[source, q], order[...], NT, preferred_element_type=F32
            ).astype(BF16)
            more = lax.dot_general(lhs[q], rhs[...], NN, preferred_element_type=F32)

            @pl.when(k == 0)
            def _():
                ints[...] = more

            @pl.when(k > 0)
            def _():
                ints[...] += more

            return c2

        lax.fori_loop(0, n_aux, step, 0)

        left = jnp.where(t == 0, v, other)
        right = jnp.where(source == 0, v, other)
        base = -(eps_down(left) + eps_across(right))
        total = jnp.zeros((width, LANES), F32)
        for ci in range(supers):
            for cj in range(ci, supers):
                turned = []
                for g in range(groups):
                    block = ints[pl.ds((cj * groups + g) * width, width), pl.ds(ci * LANES, LANES)]
                    turned.append([block if r == 0 else pltpu.roll(block, r * width, 1) for r in range(groups)])
                for s in range(groups):
                    i = ci * groups + s
                    direct = ints[pl.ds(i * width, width), pl.ds(cj * LANES, LANES)]
                    swapped = turned[0][(0 - s) % groups]
                    for g in range(1, groups):
                        swapped = jnp.where(part == g, turned[g][(g - s) % groups], swapped)
                    below = base + (occ_lane[cj] + occ_ref[i])
                    if ci == cj:
                        term = direct * (2.0 * direct - swapped) / below
                    else:
                        term = 2.0 * (direct * (direct - swapped) + swapped * swapped) / below
                    total = total + term
                    short = term[0:8]
                    for m in range(8, width, 8):
                        short = short + term[m:m + 8]
                    sums[i * 8:i * 8 + 8, cj * LANES:(cj + 1) * LANES] = short

        wide = lax.broadcasted_iota(jnp.int32, (cols, LANES), 0)
        thin = lax.broadcasted_iota(jnp.int32, (cols, LANES), 1)
        fold = jnp.where(wide // width == thin, 1.0, 0.0)
        by_j = lax.dot_general(sums[...], fold, NN, precision=EXACT, preferred_element_type=F32)
        ri = lax.broadcasted_iota(jnp.int32, (tall * 8, occ * 8), 0)
        rj = lax.broadcasted_iota(jnp.int32, (tall * 8, occ * 8), 1)
        by_ij = lax.dot_general(
            jnp.where(rj // 8 == ri, 1.0, 0.0), by_j, NN,
            precision=EXACT, preferred_element_type=F32,
        )
        packed = by_ij[0:8]
        for g in range(1, tall):
            packed = packed + pltpu.roll(by_ij[g * 8:g * 8 + 8], g * width, 1)
        pads = [jnp.zeros((free, LANES), F32), total]
        if free + width < LANES:
            pads.append(jnp.zeros((LANES - free - width, LANES), F32))
        spread = jnp.concatenate(pads, 0)
        by_row = lax.dot_general(
            jnp.ones((8, LANES), F32), spread, NT, precision=EXACT, preferred_element_type=F32)
        by_col = lax.dot_general(
            jnp.ones((8, width), F32), total, NN, precision=EXACT, preferred_element_type=F32)
        folded = by_col
        for g in range(1, groups):
            folded = folded + pltpu.roll(by_col, g * width, 1)
        half = jnp.where(diag, 0.5, 1.0)
        packed = packed * half
        both = (by_row + folded) * 0.5
        first = jnp.where(diag, jnp.where(t == 0, both, 0.0), by_row)
        second = jnp.where(diag, jnp.where(t == 1, both, 0.0), folded)
        out = jnp.where(l8 < free, packed, jnp.where(r8 == 0, first, jnp.where(r8 == 1, second, 0.0)))

        @pl.when(t == 0)
        def _():
            message[...] = out

        @pl.when(t == 1)
        def _():
            message[...] += out

        return c

    lax.fori_loop(0, n_tiles, tile, 0)

    def tell(k, c):
        t = lax.rem(me + k, n)
        pltpu.make_async_remote_copy(
            src_ref=message, dst_ref=slots.at[me],
            send_sem=msg_send, recv_sem=msg_recv,
            device_id={"virt": t // n_aux, "aux": lax.rem(t, n_aux)},
            device_id_type=MESH,
        ).start()
        return c

    lax.fori_loop(1, n, tell, 0)
    slots[me] = message[...]
    for copy in copies:
        copy.wait_send()
    everyone = slots.at[pl.ds(0, n - 1)]
    pltpu.make_async_copy(everyone, everyone, msg_send).wait()
    pltpu.make_async_copy(everyone, everyone, msg_recv).wait()

    keep = jnp.logical_or(l8 < free, r8 < 0)

    def add(k, acc):
        sv = k // n_aux
        so = virt_of(lax.rem(label_of(sv, n_virt) + pick(table, lax.rem(k, n_aux)), n_virt), n_virt)
        row0 = jnp.where(sv == v, 1.0, 0.0)
        row1 = jnp.where(so == v, 1.0, 0.0)
        weight = jnp.where(keep, 1.0, jnp.where(r8 == 0, row0, row1))
        return acc + slots[k] * weight

    done = lax.fori_loop(0, n, add, jnp.zeros((8, LANES), F32))
    share = done[0:1] + done[1:2]
    share_ref[...] = share[:, free:free + width]
    blocks = [done] + [pltpu.roll(done, LANES - g * width, 1) for g in range(1, tall)]
    square = jnp.concatenate(blocks + [jnp.zeros((LANES - 8 * tall, LANES), F32)], 0)
    square = jnp.where(lax.broadcasted_iota(jnp.int32, (LANES, LANES), 1) < occ, square, 0.0)
    pair = square + square.T
    pair_ref[...] = pair[0:occ, 0:occ]


def on_device(n_virt, n_aux, three_index, eps_occ, eps_virt):
    occ = eps_occ.shape[0]
    rows, cols = three_index.shape
    width = cols // occ
    padded = -(-rows // LANES) * LANES
    n = n_virt * n_aux
    vmem = pl.BlockSpec(memory_space=pltpu.VMEM)
    smem = pl.BlockSpec(memory_space=pltpu.SMEM)
    share, pair = pl.pallas_call(
        functools.partial(kernel, n_virt, n_aux, occ),
        out_shape=(
            jax.ShapeDtypeStruct((1, width), F32),
            jax.ShapeDtypeStruct((occ, occ), F32),
        ),
        in_specs=[vmem, smem, smem],
        out_specs=(vmem, vmem),
        scratch_shapes=[
            pltpu.VMEM((2, n_aux, rows, cols), BF16),
            pltpu.VMEM((n_aux, cols, padded), BF16),
            pltpu.VMEM((padded, cols), BF16),
            pltpu.VMEM((cols, cols), BF16),
            pltpu.VMEM((cols, cols), F32),
            pltpu.VMEM((occ * 8, cols), F32),
            pltpu.VMEM((8, LANES), F32),
            pltpu.VMEM((8, LANES), F32),
            pltpu.VMEM((n, 8, LANES), F32),
            pltpu.SemaphoreType.DMA,
            pltpu.SemaphoreType.DMA((2, n_aux)),
            pltpu.SemaphoreType.DMA((2, n_aux)),
            pltpu.SemaphoreType.DMA,
            pltpu.SemaphoreType.DMA,
        ],
        compiler_params=pltpu.CompilerParams(collective_id=0, has_side_effects=True),
    )(three_index, eps_occ, eps_virt)
    return share.reshape(width), pair


def solution(mesh):
    n_virt, n_aux = mesh.shape["virt"], mesh.shape["aux"]
    assert n_virt == 2 * n_aux
    in_specs = (P("aux", "virt"), P(), P())
    out_specs = (P("virt"), P())
    return jax.shard_map(
        functools.partial(on_device, n_virt, n_aux), mesh=mesh,
        in_specs=in_specs, out_specs=out_specs, check_vma=False,
    )
```

time: 130 us -> 48.5 us (0.37)
  blocking collectives: 64.4 us -> 0 us
  Pallas kernels: 0 us -> 45.1 us
  waiting for transfers between devices: 32.7 us -> 0 us
  between operations: 14.1 us -> 0.65 us
  other arithmetic: 6.69 us -> 0 us
  local copies, waits for them, and re-layouts: 8.83 us -> 2.48 us
  matrix products: 2.73 us -> 0 us
    psum x2 -> x0, blocking collectives: 45.4 us -> none  [the longest x1 34.8 us: on_device(): pair_energy = lax.psum(pair_column, 'virt')]
    pallas_call x0 -> x1, Pallas kernels: none -> 45.1 us  [on_device(): pl.pallas_call(functools.partial(kernel, n_virt, n_aux, occ), out_shape=(...]
    all_gather x1 -> x0, waiting for transfers between devices: 32.6 us -> none  [on_device(): partner = lax.all_gather(narrow, 'virt', axis=1, tiled=True)]
    all_to_all x1 -> x0, blocking collectives: 10.6 us -> none  [on_device(): lax.all_to_all(three_index, 'aux', split_axis=1, concat_axis=0, tiled=True)]
    all_gather x1 -> x0, blocking collectives: 8.36 us -> none  [on_device(): incoming = lax.all_gather(three_index, 'aux', axis=0, tiled=True)]
    reduce_sum x1 -> x0, other arithmetic: 6.49 us -> none  [on_device(): pair_local = jnp.sum(energy_terms, axis=(1, 3))]
    reshape x3 -> x0, local copies, waits for them, and re-layouts: 4.53 us -> none  [the longest x1 2.67 us: on_device(): partner_cube = partner.reshape(partner.shape[0], other_width, occupied)]
    dot_general x1 -> x0, matrix products: 2.73 us -> none  [on_device(): jnp.einsum('pai,pbj->iajb', left_cube, partner_cube, preferred_element_ty...]
  transfers between devices with their start and end apart: 1 -> 0, of which waited for: 1 -> 0; matrix products, arithmetic and copies ran while one was open for 3% -> 0% of each run, Pallas kernels for 0% -> 0%
where the time goes in v1:
time: 48.5 us; the launch traced here: 48.2 us
  Pallas kernels  45.1 us (93%)
  local copies, waits for them, and re-layouts  2.48 us (5%)
  between operations  0.65 us (1%)
    pallas_call x1, Pallas kernels, on_device(): pl.pallas_call(functools.partial(kernel, n_virt, n_aux, occ), out_shape=(...  45.1 us
    unnamed x4, local copies, waits for them, and re-layouts  2.48 us

profile of v1, /device:TPU:0, one launch (start us, length us, event | category | flops | bytes accessed | tf_op | source)
XLA Modules:
  0.0 48.2 jit_solution(13366684386348792743)
XLA Ops:
  0.6 45.1 %shard_map.50 = (f32[1,32]{1,0:T(1,128)}, f32[20,20]{1,0:T(8,128)}) custom-call(bf16[150,640]{1,0:T(8,128)(2,1)} %x_ref.1, f32[20]{0:T(128)} %occ_ref.1, f32[256]{0:T(256)} %virt_ref.1), custom_call_target="tpu_custom_call" | custom-call | tf_op jit(solution)/shard_map/pallas_call | solution.py:301
  45.8 0.0 copy-start
  45.8 0.7 %copy-done = f32[1,32]{1,0:T(1,128)S(1)} copy-done((f32[1,32]{1,0:T(1,128)S(1)}, f32[1,32]{1,0:T(1,128)}, u32[]{:S(2)}) %copy-start) | copy-done | bytes 152
  46.4 0.5 %copy.7 = f32[32]{0:T(128)} copy(f32[32]{0:T(128)S(1)} %bitcast.1) | data formatting | bytes 256
  46.9 1.3 %copy.8 = f32[20,20]{1,0:T(8,128)} copy(f32[20,20]{1,0:T(8,128)} %get-tuple-element.9) | data formatting | bytes 3200
Async XLA Ops:
  45.8 0.7 %copy-start = (f32[1,32]{1,0:T(1,128)S(1)}, f32[1,32]{1,0:T(1,128)}, u32[]{:S(2)}) copy-start(f32[1,32]{1,0:T(1,128)} %get-tuple-element.4) | copy-start | bytes 388

commit v2 on v1

--- a/solution.py
+++ b/solution.py
@@ -39,11 +39,12 @@
 def kernel(
     n_virt, n_aux, occ,
     x_ref, occ_ref, virt_ref,
-    share_ref, pair_ref,
-    held, lhs, rhs, order, ints, sums, parts, message, slots,
+    done_ref,
+    held, lhs, rhs, order, order_t, ints, sums, parts, message, slots,
     own_sem, send_sem, recv_sem, msg_send, msg_recv,
 ):
     rows, cols = x_ref.shape
+    pitch = -(-rows // 16) * 16
     width = cols // occ
     groups = LANES // width
     supers = occ // groups
@@ -54,7 +55,9 @@
     table = distances(n_aux)
     label = label_of(v, n_virt)
     other = virt_of(lax.rem(label + pick(table, p), n_virt), n_virt)
-    diag = jnp.logical_and(p == n_aux - 1, label >= n_virt // 2)
+    lower = label < n_virt // 2
+    solo = jnp.logical_and(p == n_aux - 1, jnp.logical_not(lower))
+    extra = jnp.logical_and(p == n_aux // 2 - 1, lower)
 
     barrier = pltpu.get_barrier_semaphore()
 
@@ -72,24 +75,42 @@
     own.start()
     pl.semaphore_wait(barrier, n - 1)
 
-    copies = []
-    for k in range(n_aux):
-        q = lax.rem(p + k, n_aux)
-        target = virt_of(lax.rem(label + n_virt - pick(table, q), n_virt), n_virt)
-        copies.append(pltpu.make_async_remote_copy(
+    pairs = n_aux // 2
+
+    def place(k):
+        return lax.rem(p // 2 + k // 2, pairs) * 2 + lax.rem(p + k, 2)
+
+    def share_own(k):
+        return pltpu.make_async_remote_copy(
+            src_ref=x_ref, dst_ref=held.at[0, p],
+            send_sem=send_sem.at[0, k], recv_sem=recv_sem.at[0, p],
+            device_id={"virt": v, "aux": place(k)}, device_id_type=MESH,
+        )
+
+    def hand_on(k):
+        q = place(k)
+        return pltpu.make_async_remote_copy(
+            src_ref=held.at[0, q], dst_ref=held.at[0, q],
+            send_sem=send_sem.at[2, k], recv_sem=recv_sem.at[0, q],
+            device_id={"virt": v, "aux": place(1)}, device_id_type=MESH,
+        )
+
+    def share_other(k):
+        q = place(k)
+        target = lax.rem(label + n_virt - pick(table, q), n_virt)
+        copy = pltpu.make_async_remote_copy(
             src_ref=x_ref, dst_ref=held.at[1, p],
             send_sem=send_sem.at[1, k], recv_sem=recv_sem.at[1, p],
-            device_id={"virt": target, "aux": q}, device_id_type=MESH,
-        ))
-    for k in range(1, n_aux):
-        q = lax.rem(p + k, n_aux)
-        copies.append(pltpu.make_async_remote_copy(
-            src_ref=x_ref, dst_ref=held.at[0, p],
-            send_sem=send_sem.at[0, k], recv_sem=recv_sem.at[0, p],
-            device_id={"virt": v, "aux": q}, device_id_type=MESH,
-        ))
-    for copy in copies:
-        copy.start()
+            device_id={"virt": virt_of(target, n_virt), "aux": q}, device_id_type=MESH,
+        )
+        wanted = jnp.logical_or(q < n_aux - 1, target < n_virt // 2)
+        return copy, wanted
+
+    for k in list(range(2, n_aux, 2)) + [1]:
+        share_own(k).start()
+    for k in range(n_aux):
+        copy, wanted = share_other(k)
+        pl.when(wanted)(copy.start)
 
     def arrived(side, q):
         pltpu.make_async_copy(
@@ -100,24 +121,25 @@
     col = lax.broadcasted_iota(jnp.int32, (cols, cols), 1)
     hit = col == lax.rem(row, width) * occ + row // width
     order[...] = jnp.where(hit, 1.0, 0.0).astype(BF16)
+    hit = row == lax.rem(col, width) * occ + col // width
+    order_t[...] = jnp.where(hit, 1.0, 0.0).astype(BF16)
     lhs[...] = jnp.zeros_like(lhs)
     rhs[...] = jnp.zeros_like(rhs)
 
-    def turn(side, q):
-        lhs[q, :, 0:rows] = lax.dot_general(
-            order[...], held[side, q], NT, preferred_element_type=F32
+    def turn(k):
+        lhs[:, k * pitch:k * pitch + rows] = lax.dot_general(
+            order[...], held[0, place(k)], NT, preferred_element_type=F32
         ).astype(BF16)
 
     own.wait()
-    turn(0, p)
-
-    def take(k, c):
-        q = lax.rem(p + k, n_aux)
-        arrived(0, q)
-        turn(0, q)
-        return c
-
-    lax.fori_loop(1, n_aux, take, 0)
+    turn(0)
+    for k in range(2, n_aux, 2):
+        arrived(0, place(k))
+        hand_on(k).start()
+        turn(k)
+    for k in range(1, n_aux, 2):
+        arrived(0, place(k))
+        turn(k)
 
     lane = lax.broadcasted_iota(jnp.int32, (1, LANES), 1)
     part = lane // width
@@ -145,46 +167,27 @@
 
     tall = -(-occ // 8)
     sums[...] = jnp.zeros_like(sums)
-    n_tiles = jnp.where(diag, 2, 1)
+    n_tiles = jnp.where(extra, 2, 1)
     r8 = lax.broadcasted_iota(jnp.int32, (8, LANES), 0)
     l8 = lax.broadcasted_iota(jnp.int32, (8, LANES), 1)
     free = tall * width
 
     def tile(t, c):
-        last = t == n_tiles - 1
-        source = jnp.where(diag, t, 1)
-
-        def step(k, c2):
-            q = lax.rem(p + k, n_aux)
-
-            @pl.when(last)
+        diag = jnp.logical_or(solo, jnp.logical_and(extra, t == 0))
+        source = jnp.where(diag, 0, 1)
+
+        for k in range(n_aux):
+
+            @pl.when(source == 1)
             def _():
-                arrived(1, q)
-
-            @pl.when(t == 1)
-            def _():
-                turn(1, q)
-
-            rhs[0:rows, :] = lax.dot_general(
-                held[source, q], order[...], NT, preferred_element_type=F32
+                arrived(1, place(k))
+
+            rhs[k * pitch:k * pitch + rows, :] = lax.dot_general(
+                held[source, place(k)], order_t[...], NN, preferred_element_type=F32
             ).astype(BF16)
-            more = lax.dot_general(lhs[q], rhs[...], NN, preferred_element_type=F32)
-
-            @pl.when(k == 0)
-            def _():
-                ints[...] = more
-
-            @pl.when(k > 0)
-            def _():
-                ints[...] += more
-
-            return c2
-
-        lax.fori_loop(0, n_aux, step, 0)
-
-        left = jnp.where(t == 0, v, other)
-        right = jnp.where(source == 0, v, other)
-        base = -(eps_down(left) + eps_across(right))
+        ints[...] = lax.dot_general(lhs[...], rhs[...], NN, preferred_element_type=F32)
+
+        base = -(eps_down(v) + eps_across(jnp.where(diag, v, other)))
         total = jnp.zeros((width, LANES), F32)
         for ci in range(supers):
             for cj in range(ci, supers):
@@ -233,11 +236,9 @@
         folded = by_col
         for g in range(1, groups):
             folded = folded + pltpu.roll(by_col, g * width, 1)
-        half = jnp.where(diag, 0.5, 1.0)
-        packed = packed * half
-        both = (by_row + folded) * 0.5
-        first = jnp.where(diag, jnp.where(t == 0, both, 0.0), by_row)
-        second = jnp.where(diag, jnp.where(t == 1, both, 0.0), folded)
+        packed = packed * jnp.where(diag, 0.5, 1.0)
+        first = jnp.where(diag, (by_row + folded) * 0.5, by_row)
+        second = jnp.where(diag, 0.0, folded)
         out = jnp.where(l8 < free, packed, jnp.where(r8 == 0, first, jnp.where(r8 == 1, second, 0.0)))
 
         @pl.when(t == 0)
@@ -264,8 +265,13 @@
 
     lax.fori_loop(1, n, tell, 0)
     slots[me] = message[...]
-    for copy in copies:
-        copy.wait_send()
+    for k in list(range(2, n_aux, 2)) + [1]:
+        share_own(k).wait_send()
+    for k in range(2, n_aux, 2):
+        hand_on(k).wait_send()
+    for k in range(n_aux):
+        copy, wanted = share_other(k)
+        pl.when(wanted)(copy.wait_send)
     everyone = slots.at[pl.ds(0, n - 1)]
     pltpu.make_async_copy(everyone, everyone, msg_send).wait()
     pltpu.make_async_copy(everyone, everyone, msg_recv).wait()
@@ -281,8 +287,15 @@
         return acc + slots[k] * weight
 
     done = lax.fori_loop(0, n, add, jnp.zeros((8, LANES), F32))
+    done_ref[...] = done
+
+
+def unpack(occ, width, done_ref, share_ref, pair_ref):
+    tall = -(-occ // 8)
+    free = tall * width
+    done = done_ref[...]
     share = done[0:1] + done[1:2]
-    share_ref[...] = share[:, free:free + width]
+    share_ref[...] = share[0, free:free + width]
     blocks = [done] + [pltpu.roll(done, LANES - g * width, 1) for g in range(1, tall)]
     square = jnp.concatenate(blocks + [jnp.zeros((LANES - 8 * tall, LANES), F32)], 0)
     square = jnp.where(lax.broadcasted_iota(jnp.int32, (LANES, LANES), 1) < occ, square, 0.0)
@@ -294,22 +307,20 @@
     occ = eps_occ.shape[0]
     rows, cols = three_index.shape
     width = cols // occ
-    padded = -(-rows // LANES) * LANES
+    pitch = -(-rows // 16) * 16
     n = n_virt * n_aux
     vmem = pl.BlockSpec(memory_space=pltpu.VMEM)
     smem = pl.BlockSpec(memory_space=pltpu.SMEM)
-    share, pair = pl.pallas_call(
+    done = pl.pallas_call(
         functools.partial(kernel, n_virt, n_aux, occ),
-        out_shape=(
-            jax.ShapeDtypeStruct((1, width), F32),
-            jax.ShapeDtypeStruct((occ, occ), F32),
-        ),
+        out_shape=jax.ShapeDtypeStruct((8, LANES), F32),
         in_specs=[vmem, smem, smem],
-        out_specs=(vmem, vmem),
+        out_specs=vmem,
         scratch_shapes=[
             pltpu.VMEM((2, n_aux, rows, cols), BF16),
-            pltpu.VMEM((n_aux, cols, padded), BF16),
-            pltpu.VMEM((padded, cols), BF16),
+            pltpu.VMEM((cols, n_aux * pitch), BF16),
+            pltpu.VMEM((n_aux * pitch, cols), BF16),
+            pltpu.VMEM((cols, cols), BF16),
             pltpu.VMEM((cols, cols), BF16),
             pltpu.VMEM((cols, cols), F32),
             pltpu.VMEM((occ * 8, cols), F32),
@@ -317,19 +328,27 @@
             pltpu.VMEM((8, LANES), F32),
             pltpu.VMEM((n, 8, LANES), F32),
             pltpu.SemaphoreType.DMA,
-            pltpu.SemaphoreType.DMA((2, n_aux)),
+            pltpu.SemaphoreType.DMA((3, n_aux)),
             pltpu.SemaphoreType.DMA((2, n_aux)),
             pltpu.SemaphoreType.DMA,
             pltpu.SemaphoreType.DMA,
         ],
         compiler_params=pltpu.CompilerParams(collective_id=0, has_side_effects=True),
     )(three_index, eps_occ, eps_virt)
-    return share.reshape(width), pair
+    return pl.pallas_call(
+        functools.partial(unpack, occ, width),
+        out_shape=(
+            jax.ShapeDtypeStruct((width,), F32),
+            jax.ShapeDtypeStruct((occ, occ), F32),
+        ),
+        in_specs=[vmem],
+        out_specs=(vmem, vmem),
+    )(done)
 
 
 def solution(mesh):
     n_virt, n_aux = mesh.shape["virt"], mesh.shape["aux"]
-    assert n_virt == 2 * n_aux
+    assert n_virt == 2 * n_aux and n_aux % 2 == 0
     in_specs = (P("aux", "virt"), P(), P())
     out_specs = (P("virt"), P())
     return jax.shard_map(

time: 48.5 us -> 38.8 us (0.80)
  Pallas kernels: 45.1 us -> 37.9 us
  local copies, waits for them, and re-layouts: 2.48 us -> 0 us
    pallas_call x1 -> x2, Pallas kernels: 45.1 us -> 37.9 us  [the longest x1 36.5 us: on_device(): pl.pallas_call(functools.partial(kernel, n_virt, n_aux, occ), out_shape=j...]
    unnamed x4 -> x0, local copies, waits for them, and re-layouts: 2.48 us -> none
where the time goes in v2:
time: 38.8 us; the launch traced here: 38.6 us
  Pallas kernels  37.9 us (98%)
  between operations  0.64 us (2%)
    pallas_call x1, Pallas kernels, on_device(): pl.pallas_call(functools.partial(kernel, n_virt, n_aux, occ), out_shape=j...  36.5 us
    pallas_call x1, Pallas kernels, on_device(): pl.pallas_call(functools.partial(unpack, occ, width), out_shape=(jax.Shap...  1.42 us

profile of v2, /device:TPU:0, one launch (start us, length us, event | category | flops | bytes accessed | tf_op | source)
XLA Modules:
  0.0 38.6 jit_solution(16628554847428697774)
XLA Ops:
  0.6 36.5 %shard_map.50.done_ref = f32[8,128]{1,0:T(8,128)} custom-call(bf16[150,640]{1,0:T(8,128)(2,1)} %x_ref.1, f32[20]{0:T(128)} %occ_ref.1, f32[256]{0:T(256)} %virt_ref.1), custom_call_target="tpu_custom_call" | custom-call | tf_op jit(solution)/shard_map/pallas_call | solution.py:314
  37.2 1.4 %shard_map.51 = (f32[32]{0:T(128)}, f32[20,20]{1,0:T(8,128)}) custom-call(f32[8,128]{1,0:T(8,128)} %shard_map.50.done_ref), custom_call_target="tpu_custom_call" | custom-call | tf_op jit(solution)/shard_map/pallas_call | solution.py:338
